TPU v7x, 256 devices: a whole 4x4x8 slice. The times are simulated.
256 devices in a mesh: ka: 128 (over z, y, x_hi, core), ga: 2 (over x_lo).
Axes of the slice: x: 4 (x_hi: 2, x_lo: 2; x = x_hi * 2 + x_lo), y: 4, z: 8, core: 2. Of those that a mesh axis runs over, the one named last changes fastest.
Arguments:
- coeffs: bfloat16 [128, 240, 2, 64, 128], P('ka', 'ga'), may hold values from -0.44921875 to 0.44921875
- neighbour: int32 [128, 3], P('ka'), may hold values from 0 to 127, as said below
- shift_id: int32 [128, 3], P('ka'), may hold values from 0 to 7
- block_map: int32 [8, 240], replicated, may hold values from 0 to 239, as said below
Outputs:
- intersection: float32 [128, 3, 2, 64, 64], P('ka', None, None, 'ga')
Inputs may be any that keep to these rules, and one draw needn't show every extreme that they name: `neighbour`: the k-points are numbered helically. The three columns of row k hold (k + 1) mod 128, (k + 16) mod 128 and (k + 64) mod 128, in an order drawn for each row. `block_map`: each row is a permutation of the 240 blocks. Block j lies in G-slice j // 120. In every row, each G-slice receives exactly 20 of its blocks from one other G-slice, exactly 10 from each of the remaining other G-slices, and the rest from itself.
All inputs are finite; a program needn't handle non-finite values.
Results may differ from a plain program's by a relative error of at most 0.0003.
Values may be sent and summed in bfloat16 or wider, within the bound.
No kernel may reach another device: no remote copies, remote signals or barrier semaphores. Data moves between devices by JAX's collectives and lax.ppermute only.
A program may use at most 128 MiB of HBM per device.

v0:
```python
import jax
import jax.numpy as jnp
from jax import lax
from jax.experimental import pallas as pl
from jax.experimental.pallas import tpu as pltpu
from jax.sharding import PartitionSpec as P


AXES = ("ka", "ga")
PLANE = 16
UNROLL = 12
CHUNKS = (48, 48, 24)
PAIR_UNROLL = 8


def gather_kernel(counts, index_ref, source_ref, *refs):
    outs, (stage, sems) = refs[: len(counts)], refs[len(counts) :]
    total = sum(counts)

    def fetch(n, carry):
        pltpu.make_async_copy(source_ref.at[index_ref[n]], stage.at[n], sems.at[0]).start()
        return carry

    lax.fori_loop(0, total, fetch, 0)
    pltpu.make_async_copy(source_ref.at[pl.ds(0, total)], stage, sems.at[0]).wait()
    first = 0
    copies = []
    for slot, (out, count) in enumerate(zip(outs, counts)):
        copies.append(
            pltpu.make_async_copy(stage.at[pl.ds(first, count)], out, sems.at[slot + 1])
        )
        first += count
    for copy in copies:
        copy.start()
    for copy in copies:
        copy.wait()


def gather_blocks(source, index, counts):
    anywhere = pl.BlockSpec(memory_space=pl.ANY)
    return pl.pallas_call(
        lambda *refs: gather_kernel(counts, *refs),
        grid_spec=pltpu.PrefetchScalarGridSpec(
            num_scalar_prefetch=1,
            grid=(),
            in_specs=[anywhere],
            out_specs=[anywhere for _ in counts],
            scratch_shapes=[
                pltpu.VMEM((sum(counts),) + source.shape[1:], source.dtype),
                pltpu.SemaphoreType.DMA((len(counts) + 1,)),
            ],
        ),
        out_shape=[jax.ShapeDtypeStruct((n,) + source.shape[1:], source.dtype) for n in counts],
        name="gather_blocks",
    )(index, source)


def contract_kernel(sizes, tasks, terms, bra_ref, ket_ref, active_ref, use_ref, *refs):
    sources, (blocks, sems) = refs[: len(sizes)], refs[-2:]
    outs = refs[-2 - tasks : -2]

    def staged(act):
        first = 0
        for slot, size in enumerate(sizes):

            @pl.when(use_ref[slot] > 0)
            def _(slot=slot, size=size, first=first):
                act(
                    pltpu.make_async_copy(
                        sources[slot], blocks.at[pl.ds(first, size)], sems.at[slot]
                    )
                )

            first += size

    staged(lambda copy: copy.start())
    staged(lambda copy: copy.wait())
    both = blocks.shape[1]
    bands = both // 2
    for task in range(tasks):

        def step(n, total, task=task):
            base = task * terms + n * UNROLL
            bra = jnp.concatenate([blocks[bra_ref[base + u]] for u in range(UNROLL)], axis=1)
            ket = jnp.concatenate([blocks[ket_ref[base + u]] for u in range(UNROLL)], axis=1)
            return total + lax.dot_general(
                bra, ket, (((1,), (1,)), ((), ())), preferred_element_type=jnp.float32
            )

        steps = jnp.where(active_ref[task] > 0, terms // UNROLL, 0)
        total = lax.fori_loop(0, steps, step, jnp.zeros((both, both), jnp.float32))
        outs[task][0] = total[:bands, :bands] + total[bands:, bands:]
        outs[task][1] = total[:bands, bands:] - total[bands:, :bands]


def contract(bra_index, ket_index, active, sources, use=None, after=()):
    tasks, terms = bra_index.shape
    use = active * len(sources) if use is None else use
    sizes = [source.shape[0] for source in sources]
    block = sources[0].shape[1:]
    bands = block[0] // 2
    anywhere = pl.BlockSpec(memory_space=pl.ANY)
    return pl.pallas_call(
        lambda *refs: contract_kernel(sizes, tasks, terms, *refs),
        grid_spec=pltpu.PrefetchScalarGridSpec(
            num_scalar_prefetch=4,
            grid=(),
            in_specs=[anywhere for _ in (*sources, *after)],
            out_specs=[pl.BlockSpec(memory_space=pltpu.VMEM)] * tasks,
            scratch_shapes=[
                pltpu.VMEM((sum(sizes),) + block, sources[0].dtype),
                pltpu.SemaphoreType.DMA((len(sizes),)),
            ],
        ),
        out_shape=[jax.ShapeDtypeStruct((2, bands, bands), jnp.float32)] * tasks,
        name="contract",
    )(
        bra_index.reshape(-1),
        ket_index.reshape(-1),
        jnp.stack(active).astype(jnp.int32),
        jnp.stack(use).astype(jnp.int32),
        *sources,
        *after,
    )


def split_kernel(source_ref, *refs):
    outs, (stage, sems) = refs[:-2], refs[-2:]
    copies, first = [], 0
    for slot, out in enumerate(outs):
        piece = stage.at[pl.ds(first, out.shape[0])]
        copies.append(
            (
                pltpu.make_async_copy(
                    source_ref.at[pl.ds(first, out.shape[0])], piece, sems.at[0, slot]
                ),
                pltpu.make_async_copy(piece, out, sems.at[1, slot]),
            )
        )
        first += out.shape[0]
    for fetch, _ in copies:
        fetch.start()
    for fetch, store in copies:
        fetch.wait()
        store.start()
    for _, store in copies:
        store.wait()


def split_blocks(source, sizes):
    anywhere = pl.BlockSpec(memory_space=pl.ANY)
    block, parts = source.shape[1:], len(sizes)
    return pl.pallas_call(
        split_kernel,
        in_specs=[anywhere],
        out_specs=[anywhere for _ in range(parts)],
        scratch_shapes=[
            pltpu.VMEM(source.shape, source.dtype),
            pltpu.SemaphoreType.DMA((2, parts)),
        ],
        out_shape=[jax.ShapeDtypeStruct((size,) + block, source.dtype) for size in sizes],
        name="split_blocks",
    )(source)


def pair_kernel(sizes, index_ref, active_ref, moved_ref, *refs):
    count = len(sizes)
    sources = refs[:count]
    start_ref, out_ref, moved, blocks, sems = refs[count], *refs[-4:]
    out_ref[...] = start_ref[...]

    @pl.when(active_ref[0] > 0)
    def _():
        copies = [pltpu.make_async_copy(moved_ref, moved, sems.at[count])]
        first = 0
        for slot, size in enumerate(sizes):
            copies.append(
                pltpu.make_async_copy(
                    sources[slot], blocks.at[pl.ds(first, size)], sems.at[slot]
                )
            )
            first += size
        for copy in copies:
            copy.start()
        for copy in copies:
            copy.wait()
        terms = moved.shape[0]

        def step(n, total):
            base = n * PAIR_UNROLL
            left = [
                jnp.concatenate(
                    [blocks[index_ref[side * terms + base + u]] for u in range(PAIR_UNROLL)],
                    axis=1,
                )
                for side in range(2)
            ]
            right = jnp.concatenate([moved[base + u] for u in range(PAIR_UNROLL)], axis=1)
            return total + lax.dot_general(
                jnp.concatenate(left, axis=0),
                right,
                (((1,), (1,)), ((), ())),
                preferred_element_type=jnp.float32,
            )

        out_ref[...] = lax.fori_loop(0, terms // PAIR_UNROLL, step, out_ref[...])


def contract_pair(index, active, moved, sources, start, after=()):
    sizes = [source.shape[0] for source in sources]
    anywhere = pl.BlockSpec(memory_space=pl.ANY)
    local = pl.BlockSpec(memory_space=pltpu.VMEM)
    return pl.pallas_call(
        lambda *refs: pair_kernel(sizes, *refs),
        grid_spec=pltpu.PrefetchScalarGridSpec(
            num_scalar_prefetch=2,
            grid=(),
            in_specs=[anywhere] + [anywhere for _ in sources] + [local] + [anywhere for _ in after],
            out_specs=local,
            scratch_shapes=[
                pltpu.VMEM(moved.shape, moved.dtype),
                pltpu.VMEM((sum(sizes),) + moved.shape[1:], moved.dtype),
                pltpu.SemaphoreType.DMA((len(sizes) + 1,)),
            ],
        ),
        out_shape=jax.ShapeDtypeStruct(start.shape, jnp.float32),
        name="contract_pair",
    )(index.reshape(-1), active.astype(jnp.int32)[None], moved, *sources, start, *after)


def products(total):
    bands = total.shape[1] // 2
    first, second = total[: 2 * bands], total[2 * bands :]
    one = jnp.stack(
        [
            first[:bands, :bands] + first[bands:, bands:],
            first[:bands, bands:] - first[bands:, :bands],
        ]
    )
    other = jnp.stack(
        [
            (second[:bands, :bands] + second[bands:, bands:]).T,
            (second[bands:, :bands] - second[:bands, bands:]).T,
        ]
    )
    return one, other


def ranks(flag):
    size = flag.shape[1]
    earlier = jnp.arange(size)[:, None] < jnp.arange(size)[None, :]
    return jnp.sum(flag[:, :, None] & earlier[None], axis=1, dtype=jnp.int32)


def compact(flag, value, count):
    rank = ranks(flag)
    hit = flag[:, None, :] & (rank[:, None, :] == jnp.arange(count)[None, :, None])
    return jnp.sum(jnp.where(hit, value[:, None, :], 0), axis=2, dtype=jnp.int32)


def step(coeffs, neighbour, shift_id, block_map):
    slab = coeffs.shape[1]
    bands, lanes = coeffs.shape[3], coeffs.shape[4]
    points, slices = lax.axis_size("ka"), lax.axis_size("ga")
    capacity = slab // 6
    k = lax.axis_index("ka")
    g = lax.axis_index("ga")
    plane_place = k % PLANE
    last = plane_place == PLANE - 1
    upward = k % 2 == 1
    stationary = (k < points // 2) == upward
    half = points // 2

    def route(target):
        pairs = []
        for point in range(points):
            for side in range(slices):
                to = target(point, side)
                if to is not None:
                    pairs.append((point * slices + side, to[0] % points * slices + to[1]))
        return pairs

    def move(array, target):
        return lax.ppermute(array, AXES, route(target))

    def moves_far(point):
        return (point < half) == (point % 2 == 0)

    own = coeffs.reshape(slab, 2 * bands, lanes)
    near = move(own, lambda p, s: (p + PLANE if p % 2 else p - PLANE, s))
    far = [
        move(piece, lambda p, s: (p + half, s) if moves_far(p) else None)
        for piece in split_blocks(own, CHUNKS)
    ]
    ring = move(own, lambda p, s: (p // PLANE * PLANE + (p - 1) % PLANE, s))

    aims = jnp.stack([(k + step) % points for step in (1, PLANE, half)])
    is_aim = neighbour[0][:, None] == aims[None, :]
    shifts = jnp.sum(jnp.where(is_aim, shift_id[0][:, None], 0), axis=0, dtype=jnp.int32)
    shifts_below = move(shifts, lambda p, s: (p + PLANE, s))
    shifts_before = move(shifts, lambda p, s: (p + 1, s))
    shifts_far = move(shifts, lambda p, s: (p + half, s))
    rows = jnp.stack(
        [
            jnp.where(last, shifts_below[0], shifts[0]),
            jnp.where(upward, shifts_below[1], shifts[1]),
            shifts[2],
            shifts_far[2],
            shifts_before[0],
        ]
    )
    picked = rows[:, None] == jnp.arange(block_map.shape[0])[None, :]
    relabel = jnp.sum(jnp.where(picked[:, :, None], block_map[None], 0), axis=1, dtype=jnp.int32)
    dest = jnp.broadcast_to(jnp.arange(relabel.shape[1], dtype=jnp.int32), relabel.shape)
    here, there = dest // slab == g, relabel // slab == g
    dest_local, source_local = dest - g * slab, relabel - g * slab
    outward = compact(here & ~there, dest_local, capacity)
    inward = compact(~here & there, source_local, capacity)
    local_bra = compact(here & there, dest_local, slab - capacity)
    local_ket = compact(here & there, source_local, slab - capacity)

    payload = jnp.concatenate(
        [
            outward[0],
            jnp.where(upward, inward[1], outward[1]),
            outward[2],
            inward[3],
            inward[4],
        ]
    )
    pay_one, pay_plane, pay_far, pay_wrap = gather_blocks(
        own, payload, (capacity, capacity, 2 * capacity, capacity)
    )
    cross_one = move(pay_one, lambda p, s: (p, 1 - s) if p % PLANE != PLANE - 1 else None)
    cross_plane = move(pay_plane, lambda p, s: (p, 1 - s))
    cross_far = move(pay_far, lambda p, s: None if moves_far(p) else (p, 1 - s))
    cross_wrap = move(
        pay_wrap, lambda p, s: (p + PLANE - 1, 1 - s) if p % PLANE == 0 else None
    )

    spots_all = jnp.arange(slab, dtype=jnp.int32)
    spots = spots_all[:capacity]
    at_plane, at_cross = slab, 2 * slab
    bra_plane = jnp.concatenate(
        [
            local_bra[1] + jnp.where(upward, at_plane, 0),
            jnp.where(upward, at_plane + outward[1], at_cross + spots),
        ]
    )
    ket_plane = jnp.concatenate(
        [
            local_ket[1] + jnp.where(upward, 0, at_plane),
            jnp.where(upward, at_cross + spots, at_plane + inward[1]),
        ]
    )
    one_early = contract(
        jnp.concatenate([local_bra[0], 2 * slab + spots])[None],
        jnp.concatenate([slab + local_ket[0], slab + inward[0]])[None],
        [~last],
        [own, ring, cross_one],
    )[0]
    here, there = here[2:4], there[2:4]
    leaving_rank = ranks(here & ~there)[1]
    coming_rank = ranks(~here & there)[0]
    with_ket = jnp.where(here[0], dest_local[2], slab + coming_rank)
    mine = g * slab + spots_all
    hit = relabel[2][None, :] == mine[:, None]
    first_partner = jnp.sum(jnp.where(hit, with_ket[None], 0), axis=1, dtype=jnp.int32)
    second_partner = lax.dynamic_slice_in_dim(
        jnp.where(there[1], source_local[3], slab + capacity + leaving_rank), g * slab, slab
    )
    at_ring, at_wrap = 2 * slab + capacity, 3 * slab + capacity
    bra_near = [bra_plane, jnp.concatenate([at_plane + local_bra[0], at_plane + outward[0]])]
    ket_near = [ket_plane, jnp.concatenate([at_ring + local_ket[0], at_wrap + spots])]
    total = jnp.zeros((4 * bands, 2 * bands), jnp.float32)
    first = 0
    after = (one_early,)
    for n, piece in enumerate(far):
        index = jnp.stack([x[first : first + piece.shape[0]] for x in (first_partner, second_partner)])
        first += piece.shape[0]
        total = contract_pair(index, stationary, piece, [own, cross_far], total, after)
        after = ()
        if n == len(far) - 2:
            plane_sum, one_late = contract(
                jnp.stack(bra_near),
                jnp.stack(ket_near),
                [True | last, last],
                [own, near, cross_plane, ring, cross_wrap],
                [True | last] * 3 + [last] * 2,
                after=(total,),
            )
            after = (plane_sum,)
    far_first, far_second = products(total)
    sent_far = move(
        far_second, lambda p, s: None if moves_far(p) else (p + half, s)
    )
    sent_down = move(
        jnp.stack([plane_sum, one_late]), lambda p, s: (p - PLANE, s) if p % 2 else None
    )
    totals = jnp.stack(
        [
            jnp.where(last, sent_down[1], one_early),
            jnp.where(upward, sent_down[0], plane_sum),
            jnp.where(stationary, far_first, sent_far),
        ]
    )
    kept_rows = bands // slices

    def part(side):
        return lax.dynamic_slice_in_dim(totals, side * kept_rows, kept_rows, 2)

    done = part(g) + move(part(1 - g), lambda p, s: (p, 1 - s))
    chosen = is_aim[:, :, None, None, None]
    return jnp.sum(jnp.where(chosen, done[None], 0.0), axis=1)[None]


def solution(mesh):
    in_specs = (P("ka", "ga", None, None, None), P("ka", None), P("ka", None), P())
    out_specs = P("ka", None, None, "ga", None)
    return jax.shard_map(step, mesh=mesh, in_specs=in_specs, out_specs=out_specs, check_vma=False)
```

profile of v0, /device:TPU:32, one launch (start us, length us, event | category | flops | bytes accessed | tf_op | source)
XLA Modules:
  0.0 179.7 jit_solution(11535962941137858705)
XLA Ops:
  0.1 1.3 select_reduce_fusion.7
  1.3 6.3 %collective-permute-start.1 = (s32[3]{0:T(128)S(1)}, s32[3]{0:T(128)S(1)}, u32[]{:S(2)}, u32[]{:S(2)}) collective-permute-start(s32[3]{0:T(128)S(1)} %get-tuple-element.33), channel_id=1, source_target_pairs={{0,128},{1,129},{2,130},{3,131},{4,132},{5,133},{6,134},{7,135},{8... | collective-permute-start | bytes 44 | tf_op jit(solution)/shard_map/ppermute | solution.py:284
  7.6 1.0 collective-permute-start
  8.7 5.3 %collective-permute-start.5 = (bf16[120,128,128]{2,1,0:T(8,128)(2,1)}, bf16[120,128,128]{2,1,0:T(8,128)(2,1)}, u32[]{:S(2)}, u32[]{:S(2)}) collective-permute-start(bf16[120,128,128]{2,1,0:T(8,128)(2,1)} %bitcast.95), channel_id=1, source_target_pairs={{0,30},{1,31},{2,0},{3,1},{4,2},{5,3},{6,4},{7,5},{8,6},{9,7},{10,... | collective-permute-start | bytes 11796488 | tf_op jit(solution)/shard_map/ppermute | solution.py:284
  13.9 1.0 collective-permute-start.3
  15.0 0.7 fusion.17
  15.7 3.4 %split_blocks.1 = (bf16[48,128,128]{2,1,0:T(8,128)(2,1)}, bf16[48,128,128]{2,1,0:T(8,128)(2,1)}, bf16[24,128,128]{2,1,0:T(8,128)(2,1)}) custom-call(bf16[120,128,128]{2,1,0:T(8,128)(2,1)} %bitcast.97), custom_call_target="tpu_custom_call" | custom-call | tf_op jit(solution)/shard_map/split_blocks/pallas_call | solution.py:153
  19.1 0.7 add_convert_fusion.refs_2_
  19.8 0.6 add_convert_fusion.1.refs_3_
  20.4 2.5 %collective-permute-start.9 = (bf16[48,128,128]{2,1,0:T(8,128)(2,1)}, bf16[48,128,128]{2,1,0:T(8,128)(2,1)S(1)}, u32[]{:S(2)}, u32[]{:S(2)}) collective-permute-start(bf16[48,128,128]{2,1,0:T(8,128)(2,1)} %get-tuple-element.18), channel_id=1, source_target_pairs={{0,128},{1,129},{4,132},{5,133},{8,136},{9,137},{12,140},{13,141},... | collective-permute-start | bytes 4718600 | tf_op jit(solution)/shard_map/ppermute | solution.py:284
  22.9 0.6 fusion.18
  26.2 0.7 slice.161
  26.8 1.4 stack.123
  28.6 0.2 convert_reduce_fusion.4
  28.8 0.8 convert_reduce_fusion.2
  29.6 0.2 select_reduce_fusion.5
  29.8 0.2 select_reduce_fusion.4
  30.0 0.6 add_bitcast_fusion.5
  30.6 0.7 concatenate.25.refs_0_
  31.2 4.4 %gather_blocks.1 = (bf16[20,128,128]{2,1,0:T(8,128)(2,1)}, bf16[20,128,128]{2,1,0:T(8,128)(2,1)}, bf16[40,128,128]{2,1,0:T(8,128)(2,1)}, bf16[20,128,128]{2,1,0:T(8,128)(2,1)}) custom-call(s32[100]{0:T(128)} %concatenate.25.refs_0_, bf16[120,128,128]{2,1,0:T(8,128)(2,1)} %bitcast.98), custom_call_target="tpu_custom_call" | custom-call | tf_op jit(solution)/shard_map/gather_blocks/pallas_call | solution.py:41
  35.6 3.4 %collective-permute-start.10 = (bf16[20,128,128]{2,1,0:T(8,128)(2,1)}, bf16[20,128,128]{2,1,0:T(8,128)(2,1)S(1)}, u32[]{:S(2)}, u32[]{:S(2)}) collective-permute-start(bf16[20,128,128]{2,1,0:T(8,128)(2,1)} %get-tuple-element.19), channel_id=1, source_target_pairs={{0,1},{1,0},{2,3},{3,2},{4,5},{5,4},{6,7},{7,6},{8,9},{9,8},{10,11... | collective-permute-start | bytes 1966088 | tf_op jit(solution)/shard_map/ppermute | solution.py:284
  39.4 0.6 slice_bitcast_fusion.3
  40.1 0.7 reshape.367.refs_0_
  40.7 0.7 collective-permute-start.8
  41.5 1.3 fusion.16
  42.8 1.1 pad_add_fusion.3
  43.9 1.2 reshape.366.refs_0_
  45.1 1.6 select_reduce_fusion
  46.8 44.0 %collective-permute-done.10.refs_6_ = bf16[20,128,128]{2,1,0:T(8,128)(2,1)S(1)} collective-permute-done((bf16[20,128,128]{2,1,0:T(8,128)(2,1)}, bf16[20,128,128]{2,1,0:T(8,128)(2,1)S(1)}, u32[]{:S(2)}, u32[]{:S(2)}) %collective-permute-start.10) | collective-permute-done | bytes 655392 | tf_op jit(solution)/shard_map/ppermute | solution.py:284
  90.8 2.4 %collective-permute-start.7 = (bf16[48,128,128]{2,1,0:T(8,128)(2,1)}, bf16[48,128,128]{2,1,0:T(8,128)(2,1)}, u32[]{:S(2)}, u32[]{:S(2)}) collective-permute-start(bf16[48,128,128]{2,1,0:T(8,128)(2,1)} %get-tuple-element.16), channel_id=1, source_target_pairs={{0,128},{1,129},{4,132},{5,133},{8,136},{9,137},{12,140},{13,141},... | collective-permute-start | bytes 4718600 | tf_op jit(solution)/shard_map/ppermute | solution.py:284
  93.2 1.3 broadcast_select_fusion.1
  94.6 0.6 add_bitcast_fusion.1
  95.2 0.6 pad_add_fusion.2
  95.8 0.5 broadcast_add_fusion.2
  96.3 2.2 %collective-permute-start.12 = (bf16[24,128,128]{2,1,0:T(8,128)(2,1)}, bf16[24,128,128]{2,1,0:T(8,128)(2,1)}, u32[]{:S(2)}, u32[]{:S(2)}) collective-permute-start(bf16[24,128,128]{2,1,0:T(8,128)(2,1)} %get-tuple-element.22), channel_id=1, source_target_pairs={{0,128},{1,129},{4,132},{5,133},{8,136},{9,137},{12,140},{13,141},... | collective-permute-start | bytes 2359304 | tf_op jit(solution)/shard_map/ppermute | solution.py:284
  98.5 0.6 reshape.365.refs_0_
  99.1 0.7 add_bitcast_fusion.2
  99.8 0.5 collective-permute-start.4
  100.4 2.1 %collective-permute-start.6 = (bf16[20,128,128]{2,1,0:T(8,128)(2,1)}, bf16[20,128,128]{2,1,0:T(8,128)(2,1)}, u32[]{:S(2)}, u32[]{:S(2)}) collective-permute-start(bf16[20,128,128]{2,1,0:T(8,128)(2,1)} %get-tuple-element.15), channel_id=1, source_target_pairs={{0,31},{1,30},{32,63},{33,62},{64,95},{65,94},{96,127},{97,126},{1... | collective-permute-start | bytes 1966088 | tf_op jit(solution)/shard_map/ppermute | solution.py:284
  102.5 1.3 add_bitcast_fusion.8
  103.8 0.7 add_bitcast_fusion.3
  104.6 0.7 pad_add_fusion
  105.2 0.7 reshape.362.refs_0_
  105.9 0.6 reshape.363.refs_1_
  106.5 1.3 pad_add_fusion.6
  107.8 0.6 stack.137.refs_3_
  108.4 7.6 %contract.2.refs_6_ = f32[2,64,64]{2,1,0:T(8,128)} custom-call(s32[120]{0:T(128)} %get-tuple-element.76.refs_0_, s32[120]{0:T(128)} %get-tuple-element.77.refs_1_, s32[1]{0:T(128)} %bitcast.35.refs_2_, s32[3]{0:T(128)} %stack.137.refs_3_, bf16[120,128,128]{2,1,0:T(8,128)(2,1)} %bitcast.99, bf16[120,128,128]{2,1,0:T(8,128)(2,1)} %collective-permute-done.5.refs_5_.refs_7_, ...), custom_call_target="tpu_custom_call" | custom-call | tf_op jit(solution)/shard_map/contract/pallas_call | solution.py:103
  116.0 0.9 copy.16
  116.9 0.7 broadcast_in_dim.194.refs_5_
  117.6 2.3 %contract_pair.3.refs_5_ = f32[256,128]{1,0:T(8,128)} custom-call(s32[96]{0:T(128)} %reshape.366.refs_0_, s32[1]{0:T(128)} %bitcast.31.refs_1_, bf16[48,128,128]{2,1,0:T(8,128)(2,1)} %copy-done.1, bf16[120,128,128]{2,1,0:T(8,128)(2,1)} %bitcast.100, bf16[40,128,128]{2,1,0:T(8,128)(2,1)} %copy-done, f32[256,128]{1,0:T(8,128)} %broadcast_in_dim.194.refs_5_, ...), custom_call_target="tpu_custom_call" | custom-call | tf_op jit(solution)/shard_map/contract_pair/pallas_call | solution.py:213
  119.9 19.1 %collective-permute-done.7.refs_2_ = bf16[48,128,128]{2,1,0:T(8,128)(2,1)} collective-permute-done((bf16[48,128,128]{2,1,0:T(8,128)(2,1)}, bf16[48,128,128]{2,1,0:T(8,128)(2,1)}, u32[]{:S(2)}, u32[]{:S(2)}) %collective-permute-start.7) | collective-permute-done | bytes 1572896 | tf_op jit(solution)/shard_map/ppermute | solution.py:284
  139.0 2.3 %contract_pair.4.refs_9_.refs_5_ = f32[256,128]{1,0:T(8,128)} custom-call(s32[96]{0:T(128)} %reshape.365.refs_0_, s32[1]{0:T(128)} %bitcast.31.refs_1_, bf16[48,128,128]{2,1,0:T(8,128)(2,1)} %collective-permute-done.7.refs_2_, bf16[120,128,128]{2,1,0:T(8,128)(2,1)} %bitcast.101, bf16[40,128,128]{2,1,0:T(8,128)(2,1)} %copy-done, f32[256,128]{1,0:T(8,128)} %contract_pair.3.refs_5_), custom_call_target="tpu_custom_call" | custom-call | tf_op jit(solution)/shard_map/contract_pair/pallas_call | solution.py:213
  141.3 3.6 %collective-permute-done.3.refs_5_ = bf16[120,128,128]{2,1,0:T(8,128)(2,1)} collective-permute-done((bf16[120,128,128]{2,1,0:T(8,128)(2,1)}, bf16[120,128,128]{2,1,0:T(8,128)(2,1)}, u32[]{:S(2)}, u32[]{:S(2)}) %collective-permute-start.3) | collective-permute-done | bytes 3932192 | tf_op jit(solution)/shard_map/ppermute | solution.py:284
  144.9 7.8 %contract.3 = (f32[2,64,64]{2,1,0:T(8,128)}, f32[2,64,64]{2,1,0:T(8,128)}) custom-call(s32[240]{0:T(256)} %reshape.362.refs_0_, s32[240]{0:T(256)} %reshape.363.refs_1_, s32[2]{0:T(128)} %add_convert_fusion.refs_2_, s32[5]{0:T(128)} %add_convert_fusion.1.refs_3_, bf16[120,128,128]{2,1,0:T(8,128)(2,1)} %bitcast.102, ...), custom_call_target="tpu_custom_call" | custom-call | tf_op jit(solution)/shard_map/contract/pallas_call | solution.py:103
  152.6 0.9 copy.15
  153.6 0.9 copy.14
  154.5 2.2 %contract_pair.5 = f32[256,128]{1,0:T(8,128)} custom-call(s32[48]{0:T(128)} %reshape.367.refs_0_, s32[1]{0:T(128)} %bitcast.31.refs_1_, bf16[24,128,128]{2,1,0:T(8,128)(2,1)} %collective-permute-done.12.refs_2_, bf16[120,128,128]{2,1,0:T(8,128)(2,1)} %bitcast.103, bf16[40,128,128]{2,1,0:T(8,128)(2,1)} %copy-done, f32[256,128]{1,0:T(8,128)} %contract_pair.4.refs_9_.refs_5_, ...), custom_call_target="tpu_custom_call" | custom-call | tf_op jit(solution)/shard_map/contract_pair/pallas_call | solution.py:213
  156.8 1.0 fusion.15
  158.1 1.3 collective-permute-start.13
  159.4 0.7 collective-permute-start.11
  160.1 12.7 %collective-permute-done.13 = f32[2,64,64]{1,2,0:T(8,128)S(1)} collective-permute-done((f32[2,64,64]{1,2,0:T(8,128)S(1)}, f32[2,64,64]{1,2,0:T(8,128)S(1)}, u32[]{:S(2)}, u32[]{:S(2)}) %collective-permute-start.13) | collective-permute-done | bytes 32800 | tf_op jit(solution)/shard_map/ppermute | solution.py:284
  173.0 1.5 collective-permute-start.14
  174.5 4.2 %collective-permute-done.14 = f32[3,2,32,64]{2,3,1,0:T(8,128)S(1)} collective-permute-done((f32[3,2,32,64]{2,3,1,0:T(8,128)S(1)}, f32[3,2,32,64]{2,3,1,0:T(8,128)S(1)}, u32[]{:S(2)}, u32[]{:S(2)}) %collective-permute-start.14) | collective-permute-done | bytes 49184 | tf_op jit(solution)/shard_map/ppermute | solution.py:284
  179.0 0.7 select_reduce_fusion.2
  (72 shorter events, 1.7 us)
Async XLA Ops:
  1.3 25.5 %collective-permute-start.2 = (s32[3]{0:T(128)S(1)}, s32[3]{0:T(128)S(1)}, u32[]{:S(2)}, u32[]{:S(2)}) collective-permute-start(s32[3]{0:T(128)S(1)} %get-tuple-element.33), channel_id=1, source_target_pairs={{0,2},{1,3},{2,4},{3,5},{4,6},{5,7},{6,8},{7,9},{8,10},{9,11},{10,... | collective-permute-start | bytes 44 | tf_op jit(solution)/shard_map/ppermute | solution.py:284
  1.3 24.8 %collective-permute-start.1 = (s32[3]{0:T(128)S(1)}, s32[3]{0:T(128)S(1)}, u32[]{:S(2)}, u32[]{:S(2)}) collective-permute-start(s32[3]{0:T(128)S(1)} %get-tuple-element.33), channel_id=1, source_target_pairs={{0,128},{1,129},{2,130},{3,131},{4,132},{5,133},{6,134},{7,135},{8... | collective-permute-start | bytes 44 | tf_op jit(solution)/shard_map/ppermute | solution.py:284
  7.6 12.7 %collective-permute-start = (s32[3]{0:T(128)S(1)}, s32[3]{0:T(128)S(1)}, u32[]{:S(2)}, u32[]{:S(2)}) collective-permute-start(s32[3]{0:T(128)S(1)} %get-tuple-element.33), channel_id=1, source_target_pairs={{0,32},{1,33},{2,34},{3,35},{4,36},{5,37},{6,38},{7,39},{8,40},{9,... | collective-permute-start | bytes 44 | tf_op jit(solution)/shard_map/ppermute | solution.py:284
  8.7 91.7 %collective-permute-start.5 = (bf16[120,128,128]{2,1,0:T(8,128)(2,1)}, bf16[120,128,128]{2,1,0:T(8,128)(2,1)}, u32[]{:S(2)}, u32[]{:S(2)}) collective-permute-start(bf16[120,128,128]{2,1,0:T(8,128)(2,1)} %bitcast.95), channel_id=1, source_target_pairs={{0,30},{1,31},{2,0},{3,1},{4,2},{5,3},{6,4},{7,5},{8,6},{9,7},{10,... | collective-permute-start | bytes 11796488 | tf_op jit(solution)/shard_map/ppermute | solution.py:284
  13.9 131.0 %collective-permute-start.3 = (bf16[120,128,128]{2,1,0:T(8,128)(2,1)}, bf16[120,128,128]{2,1,0:T(8,128)(2,1)}, u32[]{:S(2)}, u32[]{:S(2)}) collective-permute-start(bf16[120,128,128]{2,1,0:T(8,128)(2,1)} %bitcast.96), channel_id=1, source_target_pairs={{0,224},{1,225},{2,34},{3,35},{4,228},{5,229},{6,38},{7,39},{8,232... | collective-permute-start | bytes 11796488 | tf_op jit(solution)/shard_map/ppermute | solution.py:284
  14.9 14.7 %copy-start.8 = (s32[240]{0:T(256)}, s32[240]{0:T(256)S(1)}, u32[]{:S(2)}) copy-start(s32[240]{0:T(256)S(1)} %iota_subtract_fusion) | copy-start | bytes 2884
  15.7 12.7 %copy-start.6 = (s32[8,240]{1,0:T(8,128)S(1)}, s32[8,240]{1,0:T(8,128)}, u32[]{:S(2)}) copy-start(s32[8,240]{1,0:T(8,128)} %param.7) | copy-start | bytes 23044
  20.4 79.5 %collective-permute-start.9 = (bf16[48,128,128]{2,1,0:T(8,128)(2,1)}, bf16[48,128,128]{2,1,0:T(8,128)(2,1)S(1)}, u32[]{:S(2)}, u32[]{:S(2)}) collective-permute-start(bf16[48,128,128]{2,1,0:T(8,128)(2,1)} %get-tuple-element.18), channel_id=1, source_target_pairs={{0,128},{1,129},{4,132},{5,133},{8,136},{9,137},{12,140},{13,141},... | collective-permute-start | bytes 4718600 | tf_op jit(solution)/shard_map/ppermute | solution.py:284
  28.8 6.8 %copy-start.3 = (pred[5,240]{1,0:T(8,128)(4,1)}, pred[5,240]{1,0:T(8,128)(4,1)S(1)}, u32[]{:S(2)}) copy-start(pred[5,240]{1,0:T(8,128)(4,1)S(1)} %get-tuple-element.57) | copy-start | bytes 3604
  29.8 5.8 %copy-start.4 = (s32[5,20]{1,0:T(8,128)}, s32[5,20]{1,0:T(8,128)S(1)}, u32[]{:S(2)}) copy-start(s32[5,20]{1,0:T(8,128)S(1)} %select_reduce_fusion.5) | copy-start | bytes 1204
  30.0 5.6 %copy-start.5 = (s32[5,20]{1,0:T(8,128)}, s32[5,20]{1,0:T(8,128)S(1)}, u32[]{:S(2)}) copy-start(s32[5,20]{1,0:T(8,128)S(1)} %select_reduce_fusion.4) | copy-start | bytes 1204
  35.6 55.1 %collective-permute-start.10 = (bf16[20,128,128]{2,1,0:T(8,128)(2,1)}, bf16[20,128,128]{2,1,0:T(8,128)(2,1)S(1)}, u32[]{:S(2)}, u32[]{:S(2)}) collective-permute-start(bf16[20,128,128]{2,1,0:T(8,128)(2,1)} %get-tuple-element.19), channel_id=1, source_target_pairs={{0,1},{1,0},{2,3},{3,2},{4,5},{5,4},{6,7},{7,6},{8,9},{9,8},{10,11... | collective-permute-start | bytes 1966088 | tf_op jit(solution)/shard_map/ppermute | solution.py:284
  40.0 0.7 copy-start.7
  40.7 55.6 %collective-permute-start.8 = (bf16[40,128,128]{2,1,0:T(8,128)(2,1)}, bf16[40,128,128]{2,1,0:T(8,128)(2,1)S(1)}, u32[]{:S(2)}, u32[]{:S(2)}) collective-permute-start(bf16[40,128,128]{2,1,0:T(8,128)(2,1)} %get-tuple-element.17), channel_id=1, source_target_pairs={{2,3},{3,2},{6,7},{7,6},{10,11},{11,10},{14,15},{15,14},{18,19},{1... | collective-permute-start | bytes 3932168 | tf_op jit(solution)/shard_map/ppermute | solution.py:284
  90.8 17.6 %copy-start.2 = (bf16[20,128,128]{2,1,0:T(8,128)(2,1)}, bf16[20,128,128]{2,1,0:T(8,128)(2,1)S(1)}, u32[]{:S(2)}) copy-start(bf16[20,128,128]{2,1,0:T(8,128)(2,1)S(1)} %collective-permute-done.10.refs_6_) | copy-start | bytes 1966084
  90.8 48.2 %collective-permute-start.7 = (bf16[48,128,128]{2,1,0:T(8,128)(2,1)}, bf16[48,128,128]{2,1,0:T(8,128)(2,1)}, u32[]{:S(2)}, u32[]{:S(2)}) collective-permute-start(bf16[48,128,128]{2,1,0:T(8,128)(2,1)} %get-tuple-element.16), channel_id=1, source_target_pairs={{0,128},{1,129},{4,132},{5,133},{8,136},{9,137},{12,140},{13,141},... | collective-permute-start | bytes 4718600 | tf_op jit(solution)/shard_map/ppermute | solution.py:284
  96.3 19.6 %copy-start = (bf16[40,128,128]{2,1,0:T(8,128)(2,1)}, bf16[40,128,128]{2,1,0:T(8,128)(2,1)S(1)}, u32[]{:S(2)}) copy-start(bf16[40,128,128]{2,1,0:T(8,128)(2,1)S(1)} %collective-permute-done.8.refs_4_) | copy-start | bytes 3932164
  96.3 58.2 %collective-permute-start.12 = (bf16[24,128,128]{2,1,0:T(8,128)(2,1)}, bf16[24,128,128]{2,1,0:T(8,128)(2,1)}, u32[]{:S(2)}, u32[]{:S(2)}) collective-permute-start(bf16[24,128,128]{2,1,0:T(8,128)(2,1)} %get-tuple-element.22), channel_id=1, source_target_pairs={{0,128},{1,129},{4,132},{5,133},{8,136},{9,137},{12,140},{13,141},... | collective-permute-start | bytes 2359304 | tf_op jit(solution)/shard_map/ppermute | solution.py:284
  99.8 16.1 %copy-start.1 = (bf16[48,128,128]{2,1,0:T(8,128)(2,1)}, bf16[48,128,128]{2,1,0:T(8,128)(2,1)S(1)}, u32[]{:S(2)}) copy-start(bf16[48,128,128]{2,1,0:T(8,128)(2,1)S(1)} %collective-permute-done.9.refs_2_) | copy-start | bytes 4718596
  99.8 41.4 %collective-permute-start.4 = (bf16[20,128,128]{2,1,0:T(8,128)(2,1)}, bf16[20,128,128]{2,1,0:T(8,128)(2,1)}, u32[]{:S(2)}, u32[]{:S(2)}) collective-permute-start(bf16[20,128,128]{2,1,0:T(8,128)(2,1)} %get-tuple-element.14), channel_id=1, source_target_pairs={{0,1},{1,0},{2,3},{3,2},{4,5},{5,4},{6,7},{7,6},{8,9},{9,8},{10,11... | collective-permute-start | bytes 1966088 | tf_op jit(solution)/shard_map/ppermute | solution.py:284
  100.4 40.9 %collective-permute-start.6 = (bf16[20,128,128]{2,1,0:T(8,128)(2,1)}, bf16[20,128,128]{2,1,0:T(8,128)(2,1)}, u32[]{:S(2)}, u32[]{:S(2)}) collective-permute-start(bf16[20,128,128]{2,1,0:T(8,128)(2,1)} %get-tuple-element.15), channel_id=1, source_target_pairs={{0,31},{1,30},{32,63},{33,62},{64,95},{65,94},{96,127},{97,126},{1... | collective-permute-start | bytes 1966088 | tf_op jit(solution)/shard_map/ppermute | solution.py:284
  157.8 21.2 %copy-start.9 = (pred[3,3]{1,0:T(4,128)(4,1)S(1)}, pred[3,3]{1,0:T(4,128)(4,1)}, u32[]{:S(2)}) copy-start(pred[3,3]{1,0:T(4,128)(4,1)} %get-tuple-element.34) | copy-start | bytes 31
  158.1 14.7 %collective-permute-start.13 = (f32[2,64,64]{1,2,0:T(8,128)S(1)}, f32[2,64,64]{1,2,0:T(8,128)S(1)}, u32[]{:S(2)}, u32[]{:S(2)}) collective-permute-start(f32[2,64,64]{1,2,0:T(8,128)S(1)} %pad_maximum_fusion.2), channel_id=1, source_target_pairs={{2,130},{3,131},{6,134},{7,135},{10,138},{11,139},{14,142},{15,143... | collective-permute-start | bytes 98312 | tf_op jit(solution)/shard_map/ppermute | solution.py:284
  159.4 13.4 %collective-permute-start.11 = (f32[2,2,64,64]{2,3,1,0:T(8,128)S(1)}, f32[2,2,64,64]{2,3,1,0:T(8,128)S(1)}, u32[]{:S(2)}, u32[]{:S(2)}) collective-permute-start(f32[2,2,64,64]{2,3,1,0:T(8,128)S(1)} %pad_maximum_fusion.1), channel_id=1, source_target_pairs={{2,226},{3,227},{6,230},{7,231},{10,234},{11,235},{14,238},{15,239... | collective-permute-start | bytes 196616 | tf_op jit(solution)/shard_map/ppermute | solution.py:284
  173.0 5.8 %collective-permute-start.14 = (f32[3,2,32,64]{2,3,1,0:T(8,128)S(1)}, f32[3,2,32,64]{2,3,1,0:T(8,128)S(1)}, u32[]{:S(2)}, u32[]{:S(2)}) collective-permute-start(f32[3,2,32,64]{2,3,1,0:T(8,128)S(1)} %constant_dynamic-slice_fusion), channel_id=1, source_target_pairs={{0,1},{1,0},{2,3},{3,2},{4,5},{5,4},{6,7},{7,6},{8,9},{9,8},{10,11... | collective-permute-start | bytes 147464 | tf_op jit(solution)/shard_map/ppermute | solution.py:284
where the time goes:
time: 181 us; the launch traced here: 180 us
  waiting for transfers between devices  83.7 us (46%)
  starting transfers between devices  31.1 us (17%)
  Pallas kernels  29.9 us (17%)
  other arithmetic  17.6 us (10%)
  local copies, waits for them, and re-layouts  14.4 us (8%)
  between operations  3.16 us (2%)
    ppermute x15, waiting for transfers between devices, move(): return lax.ppermute(array, AXES, route(target))  83.7 us
    ppermute x15, starting transfers between devices, move(): return lax.ppermute(array, AXES, route(target))  31.1 us
    pallas_call x2, Pallas kernels, contract(): pl.pallas_call(lambda *refs: contract_kernel(sizes, tasks, terms, *refs),...  15.3 us
    pallas_call x3, Pallas kernels, contract_pair(): pl.pallas_call(lambda *refs: pair_kernel(sizes, *refs), grid_spec=pltpu.P...  6.77 us
    pallas_call x1, Pallas kernels, gather_blocks(): pl.pallas_call(lambda *refs: gather_kernel(counts, *refs), grid_spec=pltp...  4.35 us
  transfers between devices with their start and end apart: 15, of which 5 were waited for; matrix products, arithmetic and copies ran while one was open for 16% of the time, Pallas kernels for 15%

commit v1 on v0

--- a/solution.py
+++ b/solution.py
@@ -8,9 +8,9 @@
 
 AXES = ("ka", "ga")
 PLANE = 16
-UNROLL = 12
-CHUNKS = (48, 48, 24)
-PAIR_UNROLL = 8
+UNROLL = 24
+CHUNKS = (72, 48)
+PAIR_UNROLL = 24
 
 
 def gather_kernel(counts, index_ref, source_ref, *refs):

time: 181 us -> 176 us (0.972)
  the two profiles are of different devices: /device:TPU:32 before, /device:TPU:96 now
where the time goes in v1:
time: 176 us; the launch traced here: 175 us
  waiting for transfers between devices  89.2 us (51%)
  starting transfers between devices  31.3 us (18%)
  Pallas kernels  26.1 us (15%)
  local copies, waits for them, and re-layouts  14 us (8%)
  other arithmetic  11.7 us (7%)
  between operations  2.89 us (2%)
    ppermute x14, waiting for transfers between devices, move(): return lax.ppermute(array, AXES, route(target))  89.2 us
    ppermute x14, starting transfers between devices, move(): return lax.ppermute(array, AXES, route(target))  31.3 us
    pallas_call x2, Pallas kernels, contract(): pl.pallas_call(lambda *refs: contract_kernel(sizes, tasks, terms, *refs),...  13.6 us
    pallas_call x2, Pallas kernels, contract_pair(): pl.pallas_call(lambda *refs: pair_kernel(sizes, *refs), grid_spec=pltpu.P...  4.53 us
    pallas_call x1, Pallas kernels, gather_blocks(): pl.pallas_call(lambda *refs: gather_kernel(counts, *refs), grid_spec=pltp...  4.3 us
    pallas_call x1, Pallas kernels, split_blocks(): pl.pallas_call(split_kernel, in_specs=[anywhere], out_specs=[anywhere for...  3.63 us
  transfers between devices with their start and end apart: 14, of which 5 were waited for; matrix products, arithmetic and copies ran while one was open for 12% of the time, Pallas kernels for 14%

profile of v1, /device:TPU:96, one launch (start us, length us, event | category | flops | bytes accessed | tf_op | source)
XLA Modules:
  0.0 175.2 jit_solution(7986629980379599882)
XLA Ops:
  0.1 1.2 select_reduce_fusion.7
  1.3 4.5 %collective-permute-start.1 = (s32[3]{0:T(128)S(1)}, s32[3]{0:T(128)S(1)}, u32[]{:S(2)}, u32[]{:S(2)}) collective-permute-start(s32[3]{0:T(128)S(1)} %get-tuple-element.31), channel_id=1, source_target_pairs={{0,128},{1,129},{2,130},{3,131},{4,132},{5,133},{6,134},{7,135},{8... | collective-permute-start | bytes 44 | tf_op jit(solution)/shard_map/ppermute | solution.py:284
  5.8 4.6 %collective-permute-start.5 = (bf16[120,128,128]{2,1,0:T(8,128)(2,1)}, bf16[120,128,128]{2,1,0:T(8,128)(2,1)}, u32[]{:S(2)}, u32[]{:S(2)}) collective-permute-start(bf16[120,128,128]{2,1,0:T(8,128)(2,1)} %bitcast.94), channel_id=1, source_target_pairs={{0,30},{1,31},{2,0},{3,1},{4,2},{5,3},{6,4},{7,5},{8,6},{9,7},{10,... | collective-permute-start | bytes 11796488 | tf_op jit(solution)/shard_map/ppermute | solution.py:284
  10.4 1.9 %collective-permute-start.3 = (bf16[120,128,128]{2,1,0:T(8,128)(2,1)}, bf16[120,128,128]{2,1,0:T(8,128)(2,1)}, u32[]{:S(2)}, u32[]{:S(2)}) collective-permute-start(bf16[120,128,128]{2,1,0:T(8,128)(2,1)} %bitcast.95), channel_id=1, source_target_pairs={{0,224},{1,225},{2,34},{3,35},{4,228},{5,229},{6,38},{7,39},{8,232... | collective-permute-start | bytes 11796488 | tf_op jit(solution)/shard_map/ppermute | solution.py:284
  12.4 0.6 fusion.16
  13.1 3.6 %split_blocks.1 = (bf16[72,128,128]{2,1,0:T(8,128)(2,1)}, bf16[48,128,128]{2,1,0:T(8,128)(2,1)}) custom-call(bf16[120,128,128]{2,1,0:T(8,128)(2,1)} %bitcast.96), custom_call_target="tpu_custom_call" | custom-call | tf_op jit(solution)/shard_map/split_blocks/pallas_call | solution.py:153
  16.7 0.7 add_convert_fusion.refs_2_
  17.4 0.6 add_convert_fusion.1.refs_3_
  18.0 7.6 %collective-permute-start.7 = (bf16[72,128,128]{2,1,0:T(8,128)(2,1)}, bf16[72,128,128]{2,1,0:T(8,128)(2,1)}, u32[]{:S(2)}, u32[]{:S(2)}) collective-permute-start(bf16[72,128,128]{2,1,0:T(8,128)(2,1)} %get-tuple-element.15), channel_id=1, source_target_pairs={{0,128},{1,129},{4,132},{5,133},{8,136},{9,137},{12,140},{13,141},... | collective-permute-start | bytes 7077896 | tf_op jit(solution)/shard_map/ppermute | solution.py:284
  25.6 0.6 fusion.17
  28.7 0.6 slice.154
  29.3 1.3 stack.116
  30.7 0.1 select_reduce_fusion.6
  30.9 0.2 convert_reduce_fusion.4
  31.1 0.8 convert_reduce_fusion.2
  31.9 0.2 select_reduce_fusion.5
  32.1 0.2 select_reduce_fusion.4
  32.3 0.3 select_reduce_fusion
  32.7 0.5 add_bitcast_fusion.5
  33.3 0.6 slice.181
  33.8 0.6 concatenate.25.refs_0_
  34.4 4.3 %gather_blocks.1 = (bf16[20,128,128]{2,1,0:T(8,128)(2,1)}, bf16[20,128,128]{2,1,0:T(8,128)(2,1)}, bf16[40,128,128]{2,1,0:T(8,128)(2,1)}, bf16[20,128,128]{2,1,0:T(8,128)(2,1)}) custom-call(s32[100]{0:T(128)} %concatenate.25.refs_0_, bf16[120,128,128]{2,1,0:T(8,128)(2,1)} %bitcast.97), custom_call_target="tpu_custom_call" | custom-call | tf_op jit(solution)/shard_map/gather_blocks/pallas_call | solution.py:41
  38.8 3.4 %collective-permute-start.9 = (bf16[20,128,128]{2,1,0:T(8,128)(2,1)}, bf16[20,128,128]{2,1,0:T(8,128)(2,1)S(1)}, u32[]{:S(2)}, u32[]{:S(2)}) collective-permute-start(bf16[20,128,128]{2,1,0:T(8,128)(2,1)} %get-tuple-element.17), channel_id=1, source_target_pairs={{0,1},{1,0},{2,3},{3,2},{4,5},{5,4},{6,7},{7,6},{8,9},{9,8},{10,11... | collective-permute-start | bytes 1966088 | tf_op jit(solution)/shard_map/ppermute | solution.py:284
  42.2 0.7 collective-permute-start.8
  42.9 0.2 select_reduce_fusion.3
  43.1 0.6 pad_add_fusion.2
  43.8 44.4 %collective-permute-done.9.refs_6_ = bf16[20,128,128]{2,1,0:T(8,128)(2,1)S(1)} collective-permute-done((bf16[20,128,128]{2,1,0:T(8,128)(2,1)}, bf16[20,128,128]{2,1,0:T(8,128)(2,1)S(1)}, u32[]{:S(2)}, u32[]{:S(2)}) %collective-permute-start.9) | collective-permute-done | bytes 655392 | tf_op jit(solution)/shard_map/ppermute | solution.py:284
  88.2 1.4 collective-permute-start.11
  89.6 1.2 pad_add_fusion.3
  90.7 1.3 reshape.360.refs_0_
  92.1 1.3 reshape.361.refs_0_
  93.3 0.5 add_bitcast_fusion.9
  93.9 0.5 broadcast_select_fusion.1
  94.5 0.1 add_bitcast_fusion.2
  94.5 1.4 collective-permute-start.4
  96.0 2.1 %collective-permute-start.6 = (bf16[20,128,128]{2,1,0:T(8,128)(2,1)}, bf16[20,128,128]{2,1,0:T(8,128)(2,1)}, u32[]{:S(2)}, u32[]{:S(2)}) collective-permute-start(bf16[20,128,128]{2,1,0:T(8,128)(2,1)} %get-tuple-element.14), channel_id=1, source_target_pairs={{0,31},{1,30},{32,63},{33,62},{64,95},{65,94},{96,127},{97,126},{1... | collective-permute-start | bytes 1966088 | tf_op jit(solution)/shard_map/ppermute | solution.py:284
  98.1 0.1 add_bitcast_fusion.3
  98.3 0.7 reshape.357.refs_0_
  99.0 0.7 reshape.358.refs_1_
  99.6 1.3 pad_add_fusion.5
  100.9 0.5 stack.128.refs_3_
  101.5 6.7 %contract.2.refs_6_ = f32[2,64,64]{2,1,0:T(8,128)} custom-call(s32[120]{0:T(128)} %get-tuple-element.70.refs_0_, s32[120]{0:T(128)} %get-tuple-element.71.refs_1_, s32[1]{0:T(128)} %bitcast.34.refs_2_, s32[3]{0:T(128)} %stack.128.refs_3_, bf16[120,128,128]{2,1,0:T(8,128)(2,1)} %bitcast.98, bf16[120,128,128]{2,1,0:T(8,128)(2,1)} %collective-permute-done.5.refs_5_.refs_7_, ...), custom_call_target="tpu_custom_call" | custom-call | tf_op jit(solution)/shard_map/contract/pallas_call | solution.py:103
  108.2 0.9 copy.16
  109.1 0.5 collective-permute-done.7.refs_2_
  109.7 0.7 broadcast_in_dim.193.refs_5_
  110.3 2.3 %contract_pair.2.refs_9_.refs_5_ = f32[256,128]{1,0:T(8,128)} custom-call(s32[144]{0:T(256)} %reshape.360.refs_0_, s32[1]{0:T(128)} %bitcast.31.refs_1_, bf16[72,128,128]{2,1,0:T(8,128)(2,1)} %collective-permute-done.7.refs_2_, bf16[120,128,128]{2,1,0:T(8,128)(2,1)} %bitcast.99, bf16[40,128,128]{2,1,0:T(8,128)(2,1)} %copy-done, ...), custom_call_target="tpu_custom_call" | custom-call | tf_op jit(solution)/shard_map/contract_pair/pallas_call | solution.py:213
  112.6 25.1 %collective-permute-done.3.refs_5_ = bf16[120,128,128]{2,1,0:T(8,128)(2,1)} collective-permute-done((bf16[120,128,128]{2,1,0:T(8,128)(2,1)}, bf16[120,128,128]{2,1,0:T(8,128)(2,1)}, u32[]{:S(2)}, u32[]{:S(2)}) %collective-permute-start.3) | collective-permute-done | bytes 3932192 | tf_op jit(solution)/shard_map/ppermute | solution.py:284
  137.7 6.9 %contract.3 = (f32[2,64,64]{2,1,0:T(8,128)}, f32[2,64,64]{2,1,0:T(8,128)}) custom-call(s32[240]{0:T(256)} %reshape.357.refs_0_, s32[240]{0:T(256)} %reshape.358.refs_1_, s32[2]{0:T(128)} %add_convert_fusion.refs_2_, s32[5]{0:T(128)} %add_convert_fusion.1.refs_3_, bf16[120,128,128]{2,1,0:T(8,128)(2,1)} %bitcast.100, ...), custom_call_target="tpu_custom_call" | custom-call | tf_op jit(solution)/shard_map/contract/pallas_call | solution.py:103
  144.7 0.9 copy.15
  145.6 0.9 copy.14
  146.5 1.1 copy-done.1
  147.7 2.3 %contract_pair.3 = f32[256,128]{1,0:T(8,128)} custom-call(s32[96]{0:T(128)} %reshape.361.refs_0_, s32[1]{0:T(128)} %bitcast.31.refs_1_, bf16[48,128,128]{2,1,0:T(8,128)(2,1)} %copy-done.1, bf16[120,128,128]{2,1,0:T(8,128)(2,1)} %bitcast.101, bf16[40,128,128]{2,1,0:T(8,128)(2,1)} %copy-done, f32[256,128]{1,0:T(8,128)} %contract_pair.2.refs_9_.refs_5_, ...), custom_call_target="tpu_custom_call" | custom-call | tf_op jit(solution)/shard_map/contract_pair/pallas_call | solution.py:213
  150.0 1.0 fusion.15
  151.1 0.1 copy.25
  151.2 0.1 copy.26
  151.3 1.3 collective-permute-start.12
  152.6 0.7 collective-permute-start.10
  153.3 15.0 %collective-permute-done.12 = f32[2,64,64]{1,2,0:T(8,128)S(1)} collective-permute-done((f32[2,64,64]{1,2,0:T(8,128)S(1)}, f32[2,64,64]{1,2,0:T(8,128)S(1)}, u32[]{:S(2)}, u32[]{:S(2)}) %collective-permute-start.12) | collective-permute-done | bytes 32800 | tf_op jit(solution)/shard_map/ppermute | solution.py:284
  168.4 0.1 constant_dynamic-slice_fusion
  168.5 1.6 collective-permute-start.13
  170.1 4.2 %collective-permute-done.13 = f32[3,2,32,64]{2,3,1,0:T(8,128)S(1)} collective-permute-done((f32[3,2,32,64]{2,3,1,0:T(8,128)S(1)}, f32[3,2,32,64]{2,3,1,0:T(8,128)S(1)}, u32[]{:S(2)}, u32[]{:S(2)}) %collective-permute-start.13) | collective-permute-done | bytes 49184 | tf_op jit(solution)/shard_map/ppermute | solution.py:284
  174.2 0.1 dynamic-slice_add_fusion
  174.4 0.1 copy.22
  174.5 0.7 select_reduce_fusion.2
  (56 shorter events, 0.9 us)
Async XLA Ops:
  1.3 28.0 %collective-permute-start.2 = (s32[3]{0:T(128)S(1)}, s32[3]{0:T(128)S(1)}, u32[]{:S(2)}, u32[]{:S(2)}) collective-permute-start(s32[3]{0:T(128)S(1)} %get-tuple-element.31), channel_id=1, source_target_pairs={{0,2},{1,3},{2,4},{3,5},{4,6},{5,7},{6,8},{7,9},{8,10},{9,11},{10,... | collective-permute-start | bytes 44 | tf_op jit(solution)/shard_map/ppermute | solution.py:284
  1.3 27.4 %collective-permute-start.1 = (s32[3]{0:T(128)S(1)}, s32[3]{0:T(128)S(1)}, u32[]{:S(2)}, u32[]{:S(2)}) collective-permute-start(s32[3]{0:T(128)S(1)} %get-tuple-element.31), channel_id=1, source_target_pairs={{0,128},{1,129},{2,130},{3,131},{4,132},{5,133},{6,134},{7,135},{8... | collective-permute-start | bytes 44 | tf_op jit(solution)/shard_map/ppermute | solution.py:284
  5.8 12.2 %collective-permute-start = (s32[3]{0:T(128)S(1)}, s32[3]{0:T(128)S(1)}, u32[]{:S(2)}, u32[]{:S(2)}) collective-permute-start(s32[3]{0:T(128)S(1)} %get-tuple-element.31), channel_id=1, source_target_pairs={{0,32},{1,33},{2,34},{3,35},{4,36},{5,37},{6,38},{7,39},{8,40},{9,... | collective-permute-start | bytes 44 | tf_op jit(solution)/shard_map/ppermute | solution.py:284
  5.8 90.2 %collective-permute-start.5 = (bf16[120,128,128]{2,1,0:T(8,128)(2,1)}, bf16[120,128,128]{2,1,0:T(8,128)(2,1)}, u32[]{:S(2)}, u32[]{:S(2)}) collective-permute-start(bf16[120,128,128]{2,1,0:T(8,128)(2,1)} %bitcast.94), channel_id=1, source_target_pairs={{0,30},{1,31},{2,0},{3,1},{4,2},{5,3},{6,4},{7,5},{8,6},{9,7},{10,... | collective-permute-start | bytes 11796488 | tf_op jit(solution)/shard_map/ppermute | solution.py:284
  10.4 127.3 %collective-permute-start.3 = (bf16[120,128,128]{2,1,0:T(8,128)(2,1)}, bf16[120,128,128]{2,1,0:T(8,128)(2,1)}, u32[]{:S(2)}, u32[]{:S(2)}) collective-permute-start(bf16[120,128,128]{2,1,0:T(8,128)(2,1)} %bitcast.95), channel_id=1, source_target_pairs={{0,224},{1,225},{2,34},{3,35},{4,228},{5,229},{6,38},{7,39},{8,232... | collective-permute-start | bytes 11796488 | tf_op jit(solution)/shard_map/ppermute | solution.py:284
  13.1 17.6 %copy-start.3 = (s32[8,240]{1,0:T(8,128)S(1)}, s32[8,240]{1,0:T(8,128)}, u32[]{:S(2)}) copy-start(s32[8,240]{1,0:T(8,128)} %param.7) | copy-start | bytes 23044
  18.0 91.6 %collective-permute-start.7 = (bf16[72,128,128]{2,1,0:T(8,128)(2,1)}, bf16[72,128,128]{2,1,0:T(8,128)(2,1)}, u32[]{:S(2)}, u32[]{:S(2)}) collective-permute-start(bf16[72,128,128]{2,1,0:T(8,128)(2,1)} %get-tuple-element.15), channel_id=1, source_target_pairs={{0,128},{1,129},{4,132},{5,133},{8,136},{9,137},{12,140},{13,141},... | collective-permute-start | bytes 7077896 | tf_op jit(solution)/shard_map/ppermute | solution.py:284
  38.8 49.4 %collective-permute-start.9 = (bf16[20,128,128]{2,1,0:T(8,128)(2,1)}, bf16[20,128,128]{2,1,0:T(8,128)(2,1)S(1)}, u32[]{:S(2)}, u32[]{:S(2)}) collective-permute-start(bf16[20,128,128]{2,1,0:T(8,128)(2,1)} %get-tuple-element.17), channel_id=1, source_target_pairs={{0,1},{1,0},{2,3},{3,2},{4,5},{5,4},{6,7},{7,6},{8,9},{9,8},{10,11... | collective-permute-start | bytes 1966088 | tf_op jit(solution)/shard_map/ppermute | solution.py:284
  42.2 52.4 %collective-permute-start.8 = (bf16[40,128,128]{2,1,0:T(8,128)(2,1)}, bf16[40,128,128]{2,1,0:T(8,128)(2,1)S(1)}, u32[]{:S(2)}, u32[]{:S(2)}) collective-permute-start(bf16[40,128,128]{2,1,0:T(8,128)(2,1)} %get-tuple-element.16), channel_id=1, source_target_pairs={{2,3},{3,2},{6,7},{7,6},{10,11},{11,10},{14,15},{15,14},{18,19},{1... | collective-permute-start | bytes 3932168 | tf_op jit(solution)/shard_map/ppermute | solution.py:284
  88.2 13.3 %copy-start.2 = (bf16[20,128,128]{2,1,0:T(8,128)(2,1)}, bf16[20,128,128]{2,1,0:T(8,128)(2,1)S(1)}, u32[]{:S(2)}) copy-start(bf16[20,128,128]{2,1,0:T(8,128)(2,1)S(1)} %collective-permute-done.9.refs_6_) | copy-start | bytes 1966084
  88.2 58.4 %collective-permute-start.11 = (bf16[48,128,128]{2,1,0:T(8,128)(2,1)}, bf16[48,128,128]{2,1,0:T(8,128)(2,1)S(1)}, u32[]{:S(2)}, u32[]{:S(2)}) collective-permute-start(bf16[48,128,128]{2,1,0:T(8,128)(2,1)} %get-tuple-element.20), channel_id=1, source_target_pairs={{0,128},{1,129},{4,132},{5,133},{8,136},{9,137},{12,140},{13,141},... | collective-permute-start | bytes 4718600 | tf_op jit(solution)/shard_map/ppermute | solution.py:284
  94.5 13.7 %copy-start = (bf16[40,128,128]{2,1,0:T(8,128)(2,1)}, bf16[40,128,128]{2,1,0:T(8,128)(2,1)S(1)}, u32[]{:S(2)}) copy-start(bf16[40,128,128]{2,1,0:T(8,128)(2,1)S(1)} %collective-permute-done.8.refs_4_) | copy-start | bytes 3932164
  94.5 18.1 %collective-permute-start.4 = (bf16[20,128,128]{2,1,0:T(8,128)(2,1)}, bf16[20,128,128]{2,1,0:T(8,128)(2,1)}, u32[]{:S(2)}, u32[]{:S(2)}) collective-permute-start(bf16[20,128,128]{2,1,0:T(8,128)(2,1)} %get-tuple-element.13), channel_id=1, source_target_pairs={{0,1},{1,0},{2,3},{3,2},{4,5},{5,4},{6,7},{7,6},{8,9},{9,8},{10,11... | collective-permute-start | bytes 1966088 | tf_op jit(solution)/shard_map/ppermute | solution.py:284
  96.0 16.6 %collective-permute-start.6 = (bf16[20,128,128]{2,1,0:T(8,128)(2,1)}, bf16[20,128,128]{2,1,0:T(8,128)(2,1)}, u32[]{:S(2)}, u32[]{:S(2)}) collective-permute-start(bf16[20,128,128]{2,1,0:T(8,128)(2,1)} %get-tuple-element.14), channel_id=1, source_target_pairs={{0,31},{1,30},{32,63},{33,62},{64,95},{65,94},{96,127},{97,126},{1... | collective-permute-start | bytes 1966088 | tf_op jit(solution)/shard_map/ppermute | solution.py:284
  146.5 1.2 copy-start.1
  150.9 23.5 %copy-start.4 = (pred[3,3]{1,0:T(4,128)(4,1)S(1)}, pred[3,3]{1,0:T(4,128)(4,1)}, u32[]{:S(2)}) copy-start(pred[3,3]{1,0:T(4,128)(4,1)} %get-tuple-element.32) | copy-start | bytes 31
  151.3 17.0 %collective-permute-start.12 = (f32[2,64,64]{1,2,0:T(8,128)S(1)}, f32[2,64,64]{1,2,0:T(8,128)S(1)}, u32[]{:S(2)}, u32[]{:S(2)}) collective-permute-start(f32[2,64,64]{1,2,0:T(8,128)S(1)} %pad_maximum_fusion.2), channel_id=1, source_target_pairs={{2,130},{3,131},{6,134},{7,135},{10,138},{11,139},{14,142},{15,143... | collective-permute-start | bytes 98312 | tf_op jit(solution)/shard_map/ppermute | solution.py:284
  152.6 15.7 %collective-permute-start.10 = (f32[2,2,64,64]{2,3,1,0:T(8,128)S(1)}, f32[2,2,64,64]{2,3,1,0:T(8,128)S(1)}, u32[]{:S(2)}, u32[]{:S(2)}) collective-permute-start(f32[2,2,64,64]{2,3,1,0:T(8,128)S(1)} %pad_maximum_fusion.1), channel_id=1, source_target_pairs={{2,226},{3,227},{6,230},{7,231},{10,234},{11,235},{14,238},{15,239... | collective-permute-start | bytes 196616 | tf_op jit(solution)/shard_map/ppermute | solution.py:284
  168.5 5.8 %collective-permute-start.13 = (f32[3,2,32,64]{2,3,1,0:T(8,128)S(1)}, f32[3,2,32,64]{2,3,1,0:T(8,128)S(1)}, u32[]{:S(2)}, u32[]{:S(2)}) collective-permute-start(f32[3,2,32,64]{2,3,1,0:T(8,128)S(1)} %constant_dynamic-slice_fusion), channel_id=1, source_target_pairs={{0,1},{1,0},{2,3},{3,2},{4,5},{5,4},{6,7},{7,6},{8,9},{9,8},{10,11... | collective-permute-start | bytes 147464 | tf_op jit(solution)/shard_map/ppermute | solution.py:284
